TPU v7x, 32 devices: a 4x4x1 block of a 4x4x8 slice. The times are simulated.
32 devices in a mesh: dp: 1 (over z), tp: 32 (over x, y, core).
Axes of the slice: x: 4, y: 4, z: 1, core: 2. Of those that a mesh axis runs over, the one named last changes fastest.
The devices are a block of a 4x4x8 slice.
Arguments:
- x: bfloat16 [2048, 4096], P('dp')
- dy: bfloat16 [2048, 4096], P('dp')
- gate: bfloat16 [2048, 16384], P('dp', 'tp')
- up: bfloat16 [2048, 16384], P('dp', 'tp')
- w_gate: bfloat16 [4096, 16384], P(None, 'tp')
- w_up: bfloat16 [4096, 16384], P(None, 'tp')
- w_down: bfloat16 [16384, 4096], P('tp')
Outputs:
- output 1: bfloat16 [2048, 4096], P('dp')
- output 2: bfloat16 [4096, 16384], P('dp', 'tp')
- output 3: bfloat16 [4096, 16384], P('dp', 'tp')
- output 4: bfloat16 [16384, 4096], P(('dp', 'tp'))
All inputs are finite; a program needn't handle non-finite values.
Results may differ from a plain program's by a relative error of at most 0.012.
Values are sent between devices in bfloat16 or wider.
A program may use at most 768 MiB of HBM per device.

v0:
```python
import jax
import jax.numpy as jnp
from jax import lax
from jax.sharding import PartitionSpec as P


def act(gate, up):
    return jax.nn.silu(gate) * up


def solution(mesh):
    def step(x, dy, gate, up, w_gate, w_up, w_down):
        hidden, back = jax.vjp(act, gate.astype(jnp.float32), up.astype(jnp.float32))
        d_hidden = jnp.dot(dy, w_down.T, preferred_element_type=jnp.float32)
        d_gate, d_up = (g.astype(jnp.bfloat16) for g in back(d_hidden))
        term = jnp.dot(d_gate, w_gate.T, preferred_element_type=jnp.float32) + jnp.dot(d_up, w_up.T, preferred_element_type=jnp.float32)
        dx = lax.psum(term.astype(jnp.bfloat16), "tp")
        dw_gate = jnp.dot(x.T, d_gate, preferred_element_type=jnp.float32)
        dw_up = jnp.dot(x.T, d_up, preferred_element_type=jnp.float32)
        dw_down = jnp.dot(hidden.astype(jnp.bfloat16).T, dy, preferred_element_type=jnp.float32)
        return dx, *(g.astype(jnp.bfloat16) for g in (dw_gate, dw_up, dw_down))

    tokens, columns, rows = P("dp", None), P(None, "tp"), P("tp", None)
    return jax.shard_map(
        step,
        mesh=mesh,
        in_specs=(tokens, tokens, P("dp", "tp"), P("dp", "tp"), columns, columns, rows),
        out_specs=(tokens, P("dp", "tp"), P("dp", "tp"), P(("dp", "tp"), None)),
        check_vma=False,
    )
```

profile of v0, /device:TPU:97, one launch (start us, length us, event | category | flops | bytes accessed | tf_op | source)
XLA Modules:
  0.0 256.6 jit_solution(7814949431946533875)
XLA Ops:
  7.2 0.1 all-reduce.2.cloned.1.call-start
  7.2 0.0 copy-start
  7.3 17.5 %fusion.8 = (bf16[2048,512]{1,0:T(8,128)(2,1)}, f32[2048,512]{1,0:T(8,128)}) fusion(bf16[2048,512]{1,0:T(8,128)(2,1)} %param.9, bf16[2048,512]{1,0:T(8,128)(2,1)} %param.10, bf16[2048,4096]{1,0:T(8,128)(2,1)} %param.8, bf16[512,4096]{1,0:T(8,128)(2,1)} %param.13), kind=kOutput, calls=%fused_computation.18 | convolution fusion | flops 8603566080 | bytes 31457280 | tf_op jit(solution)/shard_map/dot_general | solution.py:14
  24.8 0.0 copy-done
  24.8 0.0 copy-start.1
  24.8 17.0 %fusion.11 = f32[2048,4096]{1,0:T(8,128)} fusion(bf16[2048,512]{1,0:T(8,128)(2,1)} %get-tuple-element.8, bf16[4096,512]{1,0:T(8,128)(2,1)S(1)} %copy-done), kind=kOutput, calls=%fused_computation.21 | convolution fusion | flops 8589934592 | bytes 39845888 | tf_op jit(solution)/shard_map/dot_general | solution.py:16
  41.8 0.0 copy-done.1
  41.8 23.3 %add_convert_fusion = bf16[2048,4096]{1,0:T(8,128)(2,1)} fusion(f32[2048,4096]{1,0:T(8,128)} %fusion.11, bf16[4096,512]{1,0:T(8,128)(2,1)} %param.12, f32[2048,512]{1,0:T(8,128)} %get-tuple-element.9, bf16[2048,512]{1,0:T(8,128)(2,1)S(1)} %copy-done.1), kind=kOutput, calls=%fused_computation | convolution fusion | flops 8614051840 | bytes 60817408 | tf_op jit(solution)/shard_map/dot_general | solution.py:16
  65.1 0.1 all-reduce.2.cloned.1.call-update
  65.2 14.7 %fusion = bf16[4096,512]{0,1:T(8,128)(2,1)} fusion(bf16[2048,512]{1,0:T(8,128)(2,1)} %get-tuple-element.8, bf16[2048,4096]{1,0:T(8,128)(2,1)} %param.7), kind=kOutput, calls=%fused_computation.8 | convolution fusion | flops 8592031744 | bytes 23068672 | tf_op jit(solution)/shard_map/dot_general | solution.py:18
  79.8 6.4 %copy.11 = bf16[4096,512]{1,0:T(8,128)(2,1)} copy(bf16[4096,512]{0,1:T(8,128)(2,1)} %fusion) | data formatting | bytes 8388608
  86.2 15.8 %fusion.1 = bf16[4096,512]{0,1:T(8,128)(2,1)} fusion(bf16[2048,4096]{1,0:T(8,128)(2,1)} %param.7, f32[2048,512]{1,0:T(8,128)} %get-tuple-element.9, bf16[2048,512]{1,0:T(8,128)(2,1)S(1)} %copy-done.1), kind=kOutput, calls=%fused_computation.9 | convolution fusion | flops 8599371776 | bytes 27262976 | tf_op jit(solution)/shard_map/dot_general | solution.py:19
  102.1 6.4 %copy.12 = bf16[4096,512]{1,0:T(8,128)(2,1)} copy(bf16[4096,512]{0,1:T(8,128)(2,1)} %fusion.1) | data formatting | bytes 8388608
  108.5 15.5 %convolution_convert_fusion = bf16[512,4096]{1,0:T(8,128)(2,1)} fusion(bf16[2048,4096]{1,0:T(8,128)(2,1)} %param.8, bf16[2048,512]{1,0:T(8,128)(2,1)} %param.10, bf16[2048,512]{1,0:T(8,128)(2,1)S(1)} %copy-done.1), kind=kOutput, calls=%fused_computation.5 | convolution fusion | flops 8600420352 | bytes 25165824 | tf_op jit(solution)/shard_map/dot_general | solution.py:20
  124.0 111.7 %all-reduce.2.cloned.1.call-done = bf16[2048,4096]{1,0:T(8,128)(2,1)} async-done(((bf16[2048,4096]{1,0:T(8,128)(2,1)}), bf16[2048,4096]{1,0:T(8,128)(2,1)}) %all-reduce.2.cloned.1.call-update) | async-done | bytes 16777232 | tf_op jit(solution)/shard_map/psum | solution.py:17
  235.7 14.1 %copy.14 = bf16[2048,4096]{1,0:T(8,128)(2,1)} copy(bf16[2048,4096]{1,0:T(8,128)(2,1)} %all-reduce.2.cloned.1.call-done) | data formatting | bytes 33554432
Async XLA Ops:
  7.2 228.5 %all-reduce.2.cloned.1.call-start = ((), (), s32[]{:S(2)}) async-start(), calls=%async_computation | async-start | bytes 33554432 | tf_op jit(solution)/shard_map/psum | solution.py:17
  7.2 17.5 %copy-start = (bf16[4096,512]{1,0:T(8,128)(2,1)S(1)}, bf16[4096,512]{1,0:T(8,128)(2,1)}, u32[]{:S(2)}) copy-start(bf16[4096,512]{1,0:T(8,128)(2,1)} %param.11) | copy-start | bytes 12582916
  24.8 17.0 %copy-start.1 = (bf16[2048,512]{1,0:T(8,128)(2,1)S(1)}, bf16[2048,512]{1,0:T(8,128)(2,1)}, u32[]{:S(2)}) copy-start(bf16[2048,512]{1,0:T(8,128)(2,1)} %param.9) | copy-start | bytes 6291460
Sparse Core Ops, SparseCore 0:
  65.3 170.3 all-reduce.1
where the time goes:
time: 257 us
  waiting for transfers between devices  112 us (44%)
  matrix products  104 us (40%)
  local copies, waits for them, and re-layouts  26.9 us (10%)
  between operations  14.1 us (5%)
    psum x1, waiting for transfers between devices, step(): dx = lax.psum(term.astype(jnp.bfloat16), 'tp')  112 us
    unnamed x7, local copies, waits for them, and re-layouts  26.9 us
    dot_general x1, matrix products, step(): jnp.dot(d_up, w_up.T, preferred_element_type=jnp.float32)  23.3 us
    dot_general x1, matrix products, step(): d_hidden = jnp.dot(dy, w_down.T, preferred_element_type=jnp.float32)  17.5 us
    dot_general x1, matrix products, step(): jnp.dot(d_gate, w_gate.T, preferred_element_type=jnp.float32)  17 us
    dot_general x1, matrix products, step(): dw_up = jnp.dot(x.T, d_up, preferred_element_type=jnp.float32)  15.8 us
    dot_general x1, matrix products, step(): jnp.dot(hidden.astype(jnp.bfloat16).T, dy, preferred_element_type=jnp.flo...  15.5 us
    dot_general x1, matrix products, step(): dw_gate = jnp.dot(x.T, d_gate, preferred_element_type=jnp.float32)  14.7 us
  transfers between devices with their start and end apart: 1, of which 1 were waited for; matrix products, arithmetic and copies ran while one was open for 23% of the time, Pallas kernels for 0%

commit v1 on v0

v1 whole, which is shorter than its diff:
```python
import functools
import math

import jax
import jax.numpy as jnp
from jax import lax
from jax.experimental import pallas as pl
from jax.experimental.pallas import tpu as pltpu
from jax.sharding import PartitionSpec as P

MESH = pl.DeviceIdType.MESH
F32 = jnp.float32
BF16 = jnp.bfloat16

ROWS = 256
SPLIT = 2
TILE = 256
LAG = (1, 2, 3, 4, 5, 6, 12, 14, 15, 16)
SLOTS = 4


def nt(a, b):
    return lax.dot_general(a, b, (((1,), (1,)), ((), ())), preferred_element_type=F32)


def tn(a, b):
    return lax.dot_general(a, b, (((0,), (0,)), ((), ())), preferred_element_type=F32)


def kernel(side, x, dy, gate, up, w_gate, w_up, w_down, dx, og, ou, od,
           dyb, gb, ub, dgu, hid, xb, yb, own, own2, far, mid, far2, mid2, relay2,
           w_sem, c_sem, b_sem, send, recv):
    tokens, width = dx.shape
    hidden = od.shape[0]
    half = width // 2
    cu = half // SPLIT
    cw = cu // side
    sub = ROWS // side
    chunks = tokens // ROWS
    units = chunks * SPLIT
    steps = width // TILE

    me = lax.axis_index("tp")
    core = lax.rem(me, 2)
    y = lax.rem(me // 2, side)
    xx = me // (2 * side)
    p1 = xx + core * (y - xx)
    p2 = y + core * (xx - y)

    def device(a, b):
        a, b = lax.rem(a + side, side), lax.rem(b + side, side)
        return ((a + core * (b - a)) * side + b + core * (a - b)) * 2 + core

    right, left = device(p1 + 1, p2), device(p1 - 1, p2)
    right2, left2 = device(p1, p2 + 1), device(p1, p2 - 1)
    partner = me + 1 - 2 * core

    barrier = pltpu.get_barrier_semaphore()
    peers = (partner, right, left, right2, left2)
    for peer in peers:
        pl.semaphore_signal(barrier, inc=1, device_id={"tp": peer}, device_id_type=MESH)

    def load_chunk(r):
        s = lax.rem(r, 2)
        rows = pl.ds(pl.multiple_of(r * ROWS, ROWS), ROWS)
        return (
            pltpu.make_async_copy(dy.at[rows], dyb.at[s], c_sem.at[s, 0]),
            pltpu.make_async_copy(gate.at[rows], gb.at[s], c_sem.at[s, 1]),
            pltpu.make_async_copy(up.at[rows], ub.at[s], c_sem.at[s, 2]),
        )

    def load_tile(j):
        s = lax.rem(j, 2)
        cols = pl.ds(pl.multiple_of(j * TILE, TILE), TILE)
        return (
            pltpu.make_async_copy(x.at[:, cols], xb.at[s], b_sem.at[s, 0]),
            pltpu.make_async_copy(dy.at[:, cols], yb.at[s], b_sem.at[s, 1]),
        )

    load_w = (
        pltpu.make_async_copy(w_down, od, w_sem.at[0]),
        pltpu.make_async_copy(w_gate, og, w_sem.at[1]),
        pltpu.make_async_copy(w_up, ou, w_sem.at[2]),
    )
    for c in load_chunk(0):
        c.start()
    for c in load_w:
        c.start()

    pl.semaphore_wait(barrier, len(peers))

    def rows_of(u, first=0, count=ROWS):
        return pl.ds(pl.multiple_of((u // SPLIT) * ROWS + first, math.gcd(count, 64)), count)

    def base(u, h):
        return h * half + lax.rem(u, SPLIT) * cu

    def piece(u, d):
        q = lax.rem(p1 + d, side)
        return q, pl.ds(pl.multiple_of(base(u, core) + q * cw, cw), cw)

    def ship(src, dst, stage, u, to, kind):
        pltpu.make_async_remote_copy(
            src_ref=src, dst_ref=dst, send_sem=send.at[stage, lax.rem(u, 2) if stage < 5 else 0],
            recv_sem=recv.at[kind, u],
            device_id={"tp": to}, device_id_type=MESH,
        ).start()

    def arrived(ref, kind, u):
        pltpu.make_async_copy(ref, ref, recv.at[kind, u]).wait()

    def amount(rows, cols):
        return dx.at[pl.ds(0, rows), pl.ds(0, cols)]

    def left_with(ref, stage, u):
        pltpu.make_async_copy(ref, ref, send.at[stage, lax.rem(u, 2)]).wait()

    def s0(u):
        r = u // SPLIT
        s = lax.rem(r, 2)
        rows = rows_of(u)

        @pl.when(lax.rem(u, SPLIT) == 0)
        def _():
            @pl.when(r + 1 < chunks)
            def _():
                for c in load_chunk(r + 1):
                    c.start()

            for c in load_chunk(r):
                c.wait()

            @pl.when(r == 0)
            def _():
                load_w[0].wait()

            dh = nt(dyb[s], od[...])
            g = gb[s].astype(F32)
            v = ub[s].astype(F32)
            sig = jax.nn.sigmoid(g)
            silu = g * sig
            hid[:, pl.ds(pl.multiple_of(r * ROWS, ROWS), ROWS)] = (silu * v).T.astype(BF16)
            dgu[rows, hidden:] = (dh * silu).astype(BF16)
            dgu[rows, :hidden] = (dh * v * (sig + silu * (1.0 - sig))).astype(BF16)

            @pl.when(r == 0)
            def _():
                load_w[1].wait()
                load_w[2].wait()

        def term(h):
            cols = pl.ds(pl.multiple_of(base(u, h), cu), cu)
            return nt(dgu[rows, :hidden], og[cols, :]) + nt(dgu[rows, hidden:], ou[cols, :])

        there = dx.at[rows, pl.ds(pl.multiple_of(base(u, 1 - core), cu), cu)]
        there[...] = term(1 - core).astype(BF16)
        ship(there, there, 0, u, partner, 0)
        own[lax.rem(u, SLOTS)] = term(core)

    hr = ROWS // 2

    def s1(u):
        here = dx.at[rows_of(u), pl.ds(pl.multiple_of(base(u, core), cu), cu)]
        arrived(here, 0, u)
        left_with(amount(ROWS, cu), 0, u)
        mine = own.at[lax.rem(u, SLOTS)]
        upper, lower = rows_of(u, 0, hr), rows_of(u, hr, hr)

        def total(d):
            q, cols = piece(u, d)
            at = pl.ds(pl.multiple_of(q * cw, cw), cw)
            return at, cols, mine[:, at] + dx[rows_of(u), cols].astype(F32)

        at, cols, v = total(side // 2)
        dx[rows_of(u), cols] = v.astype(BF16)
        ship(dx.at[upper, cols], far.at[u, 0], 1, u, left, 1)
        ship(dx.at[lower, cols], far.at[u, 1], 1, u, right, 1)
        at, cols, v = total(1)
        dx[upper, cols] = v[:hr].astype(BF16)
        ship(dx.at[upper, cols], mid.at[u, 0], 1, u, right, 2)
        mine[hr:, at] = v[hr:]
        at, cols, v = total(side - 1)
        dx[lower, cols] = v[hr:].astype(BF16)
        ship(dx.at[lower, cols], mid.at[u, 1], 1, u, left, 2)
        mine[:hr, at] = v[:hr]
        at, cols, v = total(0)
        mine[:, at] = v

    def s2(u):
        arrived(far.at[u], 1, u)
        left_with(amount(2 * ROWS, cw), 1, u)
        mine = own.at[lax.rem(u, SLOTS)]
        upper, lower = rows_of(u, 0, hr), rows_of(u, hr, hr)
        q, cols = piece(u, side - 1)
        at = pl.ds(pl.multiple_of(q * cw, cw), cw)
        dx[upper, cols] = (mine[:hr, at] + far[u, 0].astype(F32)).astype(BF16)
        ship(dx.at[upper, cols], mid.at[u, 2], 2, u, left, 2)
        q, cols = piece(u, 1)
        at = pl.ds(pl.multiple_of(q * cw, cw), cw)
        dx[lower, cols] = (mine[hr:, at] + far[u, 1].astype(F32)).astype(BF16)
        ship(dx.at[lower, cols], mid.at[u, 3], 2, u, right, 2)

    hs = sub // 2

    def part(d):
        return pl.multiple_of(lax.rem(p2 + d, side) * sub, sub)

    def s3(u):
        arrived(mid.at[u], 2, u)
        left_with(amount(ROWS, cw), 2, u)
        q, cols = piece(u, 0)
        at = pl.ds(pl.multiple_of(q * cw, cw), cw)
        mine = own.at[lax.rem(u, SLOTS)]
        keep = own2.at[lax.rem(u, SLOTS)]
        keep[:hr] = mine[:hr, at] + mid[u, 0].astype(F32) + mid[u, 2].astype(F32)
        keep[hr:] = mine[hr:, at] + mid[u, 1].astype(F32) + mid[u, 3].astype(F32)

        f = part(side // 2)
        dx[rows_of(u, f, sub), cols] = keep[pl.ds(f, sub)].astype(BF16)
        ship(dx.at[rows_of(u, f, hs), cols], far2.at[u, 0], 3, u, left2, 3)
        ship(dx.at[rows_of(u, f + hs, hs), cols], far2.at[u, 1], 3, u, right2, 3)
        f = part(1)
        dx[rows_of(u, f, hs), cols] = keep[pl.ds(f, hs)].astype(BF16)
        ship(dx.at[rows_of(u, f, hs), cols], mid2.at[u, 0], 3, u, right2, 4)
        f = pl.multiple_of(part(side - 1) + hs, hs)
        dx[rows_of(u, f, hs), cols] = keep[pl.ds(f, hs)].astype(BF16)
        ship(dx.at[rows_of(u, f, hs), cols], mid2.at[u, 1], 3, u, left2, 4)

    def s4(u):
        arrived(far2.at[u], 3, u)
        left_with(amount(2 * sub, cw), 3, u)
        keep = own2.at[lax.rem(u, SLOTS)]
        f = part(side - 1)
        relay2[u, 0] = (keep[pl.ds(f, hs)] + far2[u, 0].astype(F32)).astype(BF16)
        ship(relay2.at[u, 0], mid2.at[u, 2], 4, u, left2, 4)
        f = pl.multiple_of(part(1) + hs, hs)
        relay2[u, 1] = (keep[pl.ds(f, hs)] + far2[u, 1].astype(F32)).astype(BF16)
        ship(relay2.at[u, 1], mid2.at[u, 3], 4, u, right2, 4)

    def s5(u):
        arrived(mid2.at[u], 4, u)
        left_with(amount(sub, cw), 4, u)
        _, cols = piece(u, 0)
        keep = own2.at[lax.rem(u, SLOTS)]
        f = part(0)
        a = keep[pl.ds(f, hs)] + mid2[u, 0].astype(F32) + mid2[u, 2].astype(F32)
        g = pl.multiple_of(f + hs, hs)
        b = keep[pl.ds(g, hs)] + mid2[u, 1].astype(F32) + mid2[u, 3].astype(F32)
        dx[rows_of(u, f, hs), cols] = a.astype(BF16)
        dx[rows_of(u, g, hs), cols] = b.astype(BF16)
        done = dx.at[rows_of(u, f, sub), cols]
        ship(done, done, 5, u, left2, 5)
        ship(done, done, 5, u, right2, 5)

    def s6(u):
        arrived(amount(2 * sub, cw), 5, u)
        _, cols = piece(u, 0)
        a = dx.at[rows_of(u, part(side - 1), hs), cols]
        b = dx.at[rows_of(u, part(1) + hs, hs), cols]
        ship(a, a, 6, u, right2, 6)
        ship(b, b, 6, u, left2, 6)

    def s7(u):
        arrived(amount(sub, cw), 6, u)
        _, cols = piece(u, 0)
        done = dx.at[rows_of(u), cols]
        ship(done, done, 7, u, left, 7)
        ship(done, done, 7, u, right, 7)
        ship(done, done, 7, u, partner, 9)

    def s8(u):
        arrived(amount(2 * ROWS, cw), 7, u)
        _, lcols = piece(u, side - 1)
        _, rcols = piece(u, 1)
        a = dx.at[rows_of(u, 0, hr), lcols]
        b = dx.at[rows_of(u, hr, hr), rcols]
        ship(a, a, 8, u, right, 8)
        ship(b, b, 8, u, left, 8)
        for cols in (lcols, rcols):
            done = dx.at[rows_of(u), cols]
            ship(done, done, 8, u, partner, 9)

    def s9(u):
        arrived(amount(ROWS, cw), 8, u)
        _, cols = piece(u, side // 2)
        done = dx.at[rows_of(u), cols]
        ship(done, done, 9, u, partner, 9)

    def s10(u):
        arrived(amount(ROWS, cu), 9, u)

    def grads(j):
        s = lax.rem(j, 2)

        @pl.when(j + 1 < steps)
        def _():
            for c in load_tile(j + 1):
                c.start()

        for c in load_tile(j):
            c.wait()
        at = pl.ds(pl.multiple_of(j * TILE, TILE), TILE)
        both = tn(xb[s], dgu[...])
        og[at, :] = both[:, :hidden].astype(BF16)
        ou[at, :] = both[:, hidden:].astype(BF16)
        od[:, at] = jnp.dot(hid[...], yb[s], preferred_element_type=F32).astype(BF16)

    total = units + max(LAG[-1], steps)

    def iteration(i, carry):
        pl.when(i < units)(lambda: s0(i))
        for lag, stage in zip(LAG, (s1, s2, s3, s4, s5, s6, s7, s8, s9, s10)):
            pl.when((i >= lag) & (i < units + lag))(functools.partial(stage, i - lag))

        @pl.when(i == units // 2)
        def _():
            for c in load_tile(0):
                c.start()

        pl.when((i >= units) & (i < units + steps))(lambda: grads(i - units))
        return carry

    lax.fori_loop(0, total, iteration, 0)

    for stage, share in ((5, 2), (6, 1), (7, 12), (8, 12), (9, 4)):
        ref = dx.at[:, pl.ds(0, share * width // 32)]
        pltpu.make_async_copy(ref, ref, send.at[stage, 0]).wait()


def solution(mesh):
    side = math.isqrt(mesh.shape["tp"] // 2)

    def step(x, dy, gate, up, w_gate, w_up, w_down):
        tokens, width = x.shape
        hidden = gate.shape[1]
        units = tokens // ROWS * SPLIT
        cu = width // 2 // SPLIT
        cw = cu // side
        sub = ROWS // side
        out = [pltpu.VMEM(a.shape, a.dtype) for a in (x, w_gate, w_up, w_down)]
        dma = pltpu.SemaphoreType.DMA
        return tuple(pl.pallas_call(
            functools.partial(kernel, side),
            out_shape=out,
            in_specs=[pl.BlockSpec(memory_space=pl.ANY)] * 7,
            out_specs=[pl.BlockSpec(memory_space=pltpu.VMEM)] * 4,
            scratch_shapes=[
                pltpu.VMEM((2, ROWS, width), BF16),
                pltpu.VMEM((2, ROWS, hidden), BF16),
                pltpu.VMEM((2, ROWS, hidden), BF16),
                pltpu.VMEM((tokens, 2 * hidden), BF16),
                pltpu.VMEM((hidden, tokens), BF16),
                pltpu.VMEM((2, tokens, TILE), BF16),
                pltpu.VMEM((2, tokens, TILE), BF16),
                pltpu.VMEM((SLOTS, ROWS, cu), F32),
                pltpu.VMEM((SLOTS, ROWS, cw), F32),
                pltpu.VMEM((units, 2, ROWS // 2, cw), BF16),
                pltpu.VMEM((units, 4, ROWS // 2, cw), BF16),
                pltpu.VMEM((units, 2, sub // 2, cw), BF16),
                pltpu.VMEM((units, 4, sub // 2, cw), BF16),
                pltpu.VMEM((units, 2, sub // 2, cw), BF16),
                dma((3,)),
                dma((2, 3)),
                dma((2, 2)),
                dma((10, 2)),
                dma((10, units)),
            ],
            compiler_params=pltpu.CompilerParams(
                collective_id=0, has_side_effects=True, vmem_limit_bytes=34 * 2**20,
            ),
        )(x, dy, gate, up, w_gate, w_up, w_down))

    tokens, columns, rows = P("dp", None), P(None, "tp"), P("tp", None)
    return jax.shard_map(
        step,
        mesh=mesh,
        in_specs=(tokens, tokens, P("dp", "tp"), P("dp", "tp"), columns, columns, rows),
        out_specs=(tokens, P("dp", "tp"), P("dp", "tp"), P(("dp", "tp"), None)),
        check_vma=False,
    )
```

time: 257 us -> 156 us (0.61)
  Pallas kernels: 0 us -> 143 us
  waiting for transfers between devices: 112 us -> 0 us
  matrix products: 104 us -> 0 us
  local copies, waits for them, and re-layouts: 26.9 us -> 12.2 us
  between operations: 14.1 us -> 0.64 us
    pallas_call x0 -> x1, Pallas kernels: none -> 143 us  [step(): pl.pallas_call(functools.partial(kernel, side), out_shape=out, in_specs=[...]
    psum x1 -> x0, waiting for transfers between devices: 112 us -> none  [step(): dx = lax.psum(term.astype(jnp.bfloat16), 'tp')]
    dot_general x6 -> x0, matrix products: 104 us -> none  [the longest x1 23.3 us: step(): jnp.dot(d_up, w_up.T, preferred_element_type=jnp.float32)]
    unnamed x7 -> x4, local copies, waits for them, and re-layouts: 26.9 us -> 12.2 us
  transfers between devices with their start and end apart: 1 -> 0, of which waited for: 1 -> 0; matrix products, arithmetic and copies ran while one was open for 23% -> 0% of each run, Pallas kernels for 0% -> 0%
where the time goes in v1:
time: 156 us
  Pallas kernels  143 us (92%)
  local copies, waits for them, and re-layouts  12.2 us (8%)
    pallas_call x1, Pallas kernels, step(): pl.pallas_call(functools.partial(kernel, side), out_shape=out, in_specs=[...  143 us
    unnamed x4, local copies, waits for them, and re-layouts  12.2 us

profile of v1, /device:TPU:97, one launch (start us, length us, event | category | flops | bytes accessed | tf_op | source)
XLA Modules:
  0.0 156.3 jit_solution(9797839474995109317)
XLA Ops:
  0.6 143.5 %shard_map.102 = (bf16[2048,4096]{1,0:T(8,128)(2,1)S(1)}, bf16[4096,512]{1,0:T(8,128)(2,1)S(1)}, bf16[4096,512]{1,0:T(8,128)(2,1)S(1)}, bf16[512,4096]{1,0:T(8,128)(2,1)S(1)}) custom-call(bf16[2048,4096]{1,0:T(8,128)(2,1)} %x.1, bf16[2048,4096]{1,0:T(8,128)(2,1)} %dy.1, bf16[2048,512]{1,0:T(8,128)(2,1)} %gate.1, bf16[2048,512]{1,0:T(8,128)(2,1)} %up.1, ...), custom_call_target="tpu_custom_call" | custom-call | tf_op jit(solution)/shard_map/pallas_call | solution.py:342
  144.1 6.2 %copy.15 = bf16[2048,4096]{1,0:T(8,128)(2,1)} copy(bf16[2048,4096]{1,0:T(8,128)(2,1)S(1)} %get-tuple-element.4) | data formatting | bytes 33554432
  150.3 2.0 %copy.16 = bf16[4096,512]{1,0:T(8,128)(2,1)} copy(bf16[4096,512]{1,0:T(8,128)(2,1)S(1)} %get-tuple-element.5) | data formatting | bytes 8388608
  152.3 2.0 %copy.17 = bf16[4096,512]{1,0:T(8,128)(2,1)} copy(bf16[4096,512]{1,0:T(8,128)(2,1)S(1)} %get-tuple-element.6) | data formatting | bytes 8388608
  154.3 2.0 %copy.18 = bf16[512,4096]{1,0:T(8,128)(2,1)} copy(bf16[512,4096]{1,0:T(8,128)(2,1)S(1)} %get-tuple-element.7) | data formatting | bytes 8388608

commit v2 on v1

--- a/solution.py
+++ b/solution.py
@@ -15,8 +15,11 @@
 ROWS = 256
 SPLIT = 2
 TILE = 256
-LAG = (1, 2, 3, 4, 5, 6, 12, 14, 15, 16)
-SLOTS = 4
+LAG = (1, 3, 5, 7, 9, 11, 14, 19, 23, 24)
+SLOTS = 5
+SLOTS2 = 5
+PUT = 4
+FLIGHT = 4
 
 
 def nt(a, b):
@@ -77,23 +80,29 @@
             pltpu.make_async_copy(dy.at[:, cols], yb.at[s], b_sem.at[s, 1]),
         )
 
-    load_w = (
-        pltpu.make_async_copy(w_down, od, w_sem.at[0]),
-        pltpu.make_async_copy(w_gate, og, w_sem.at[1]),
-        pltpu.make_async_copy(w_up, ou, w_sem.at[2]),
-    )
+    def base(u, h):
+        return h * half + lax.rem(u, SPLIT) * cu
+
+    load_down = pltpu.make_async_copy(w_down, od, w_sem.at[0])
+
+    def load_block(k, h):
+        rows = pl.ds(pl.multiple_of(base(k, core + h * (1 - 2 * core)), cu), cu)
+        at = 1 + 2 * (2 * k + h)
+        return (
+            pltpu.make_async_copy(w_gate.at[rows], og.at[rows], w_sem.at[at]),
+            pltpu.make_async_copy(w_up.at[rows], ou.at[rows], w_sem.at[at + 1]),
+        )
+
+    load_down.start()
     for c in load_chunk(0):
         c.start()
-    for c in load_w:
-        c.start()
-
-    pl.semaphore_wait(barrier, len(peers))
+    for k in range(SPLIT):
+        for h in (1, 0):
+            for c in load_block(k, h):
+                c.start()
 
     def rows_of(u, first=0, count=ROWS):
         return pl.ds(pl.multiple_of((u // SPLIT) * ROWS + first, math.gcd(count, 64)), count)
-
-    def base(u, h):
-        return h * half + lax.rem(u, SPLIT) * cu
 
     def piece(u, d):
         q = lax.rem(p1 + d, side)
@@ -101,7 +110,7 @@
 
     def ship(src, dst, stage, u, to, kind):
         pltpu.make_async_remote_copy(
-            src_ref=src, dst_ref=dst, send_sem=send.at[stage, lax.rem(u, 2) if stage < 5 else 0],
+            src_ref=src, dst_ref=dst, send_sem=send.at[stage, lax.rem(u, FLIGHT) if stage < 5 else 0],
             recv_sem=recv.at[kind, u],
             device_id={"tp": to}, device_id_type=MESH,
         ).start()
@@ -113,49 +122,53 @@
         return dx.at[pl.ds(0, rows), pl.ds(0, cols)]
 
     def left_with(ref, stage, u):
-        pltpu.make_async_copy(ref, ref, send.at[stage, lax.rem(u, 2)]).wait()
-
-    def s0(u):
+        pltpu.make_async_copy(ref, ref, send.at[stage, lax.rem(u, FLIGHT)]).wait()
+
+    def s0_hidden(u):
         r = u // SPLIT
         s = lax.rem(r, 2)
         rows = rows_of(u)
-
-        @pl.when(lax.rem(u, SPLIT) == 0)
+        for c in load_chunk(r):
+            c.wait()
+
+        @pl.when(r == 0)
         def _():
-            @pl.when(r + 1 < chunks)
+            load_down.wait()
+
+        dh = nt(dyb[s], od[...])
+        g = gb[s].astype(F32)
+        v = ub[s].astype(F32)
+        sig = jax.nn.sigmoid(g)
+        silu = g * sig
+        hid[:, pl.ds(pl.multiple_of(r * ROWS, ROWS), ROWS)] = (silu * v).T.astype(BF16)
+        dgu[rows, hidden:] = (dh * silu).astype(BF16)
+        dgu[rows, :hidden] = (dh * v * (sig + silu * (1.0 - sig))).astype(BF16)
+
+    def s0_term(u, h):
+        for k in range(SPLIT):
+            @pl.when(u == k)
             def _():
-                for c in load_chunk(r + 1):
-                    c.start()
-
-            for c in load_chunk(r):
-                c.wait()
-
-            @pl.when(r == 0)
-            def _():
-                load_w[0].wait()
-
-            dh = nt(dyb[s], od[...])
-            g = gb[s].astype(F32)
-            v = ub[s].astype(F32)
-            sig = jax.nn.sigmoid(g)
-            silu = g * sig
-            hid[:, pl.ds(pl.multiple_of(r * ROWS, ROWS), ROWS)] = (silu * v).T.astype(BF16)
-            dgu[rows, hidden:] = (dh * silu).astype(BF16)
-            dgu[rows, :hidden] = (dh * v * (sig + silu * (1.0 - sig))).astype(BF16)
-
-            @pl.when(r == 0)
-            def _():
-                load_w[1].wait()
-                load_w[2].wait()
-
-        def term(h):
-            cols = pl.ds(pl.multiple_of(base(u, h), cu), cu)
-            return nt(dgu[rows, :hidden], og[cols, :]) + nt(dgu[rows, hidden:], ou[cols, :])
-
-        there = dx.at[rows, pl.ds(pl.multiple_of(base(u, 1 - core), cu), cu)]
-        there[...] = term(1 - core).astype(BF16)
+                for c in load_block(k, h):
+                    c.wait()
+
+        rows = rows_of(u)
+        cols = pl.ds(pl.multiple_of(base(u, core + h * (1 - 2 * core)), cu), cu)
+        return nt(dgu[rows, :hidden], og[cols, :]) + nt(dgu[rows, hidden:], ou[cols, :])
+
+    def s0_first(u):
+        pl.when(lax.rem(u, SPLIT) == 0)(lambda: s0_hidden(u))
+        there = dx.at[rows_of(u), pl.ds(pl.multiple_of(base(u, 1 - core), cu), cu)]
+        there[...] = s0_term(u, 1).astype(BF16)
+        pl.when(u == 0)(lambda: pl.semaphore_wait(barrier, len(peers)))
         ship(there, there, 0, u, partner, 0)
-        own[lax.rem(u, SLOTS)] = term(core)
+
+    def s0_second(u):
+        @pl.when((lax.rem(u, SPLIT) == 0) & (u // SPLIT + 1 < chunks))
+        def _():
+            for c in load_chunk(u // SPLIT + 1):
+                c.start()
+
+        own[lax.rem(u, SLOTS)] = s0_term(u, 0)
 
     hr = ROWS // 2
 
@@ -211,7 +224,7 @@
         q, cols = piece(u, 0)
         at = pl.ds(pl.multiple_of(q * cw, cw), cw)
         mine = own.at[lax.rem(u, SLOTS)]
-        keep = own2.at[lax.rem(u, SLOTS)]
+        keep = own2.at[lax.rem(u, SLOTS2)]
         keep[:hr] = mine[:hr, at] + mid[u, 0].astype(F32) + mid[u, 2].astype(F32)
         keep[hr:] = mine[hr:, at] + mid[u, 1].astype(F32) + mid[u, 3].astype(F32)
 
@@ -229,7 +242,7 @@
     def s4(u):
         arrived(far2.at[u], 3, u)
         left_with(amount(2 * sub, cw), 3, u)
-        keep = own2.at[lax.rem(u, SLOTS)]
+        keep = own2.at[lax.rem(u, SLOTS2)]
         f = part(side - 1)
         relay2[u, 0] = (keep[pl.ds(f, hs)] + far2[u, 0].astype(F32)).astype(BF16)
         ship(relay2.at[u, 0], mid2.at[u, 2], 4, u, left2, 4)
@@ -241,7 +254,7 @@
         arrived(mid2.at[u], 4, u)
         left_with(amount(sub, cw), 4, u)
         _, cols = piece(u, 0)
-        keep = own2.at[lax.rem(u, SLOTS)]
+        keep = own2.at[lax.rem(u, SLOTS2)]
         f = part(0)
         a = keep[pl.ds(f, hs)] + mid2[u, 0].astype(F32) + mid2[u, 2].astype(F32)
         g = pl.multiple_of(f + hs, hs)
@@ -308,9 +321,11 @@
     total = units + max(LAG[-1], steps)
 
     def iteration(i, carry):
-        pl.when(i < units)(lambda: s0(i))
+        pl.when(i < units)(lambda: s0_first(i))
         for lag, stage in zip(LAG, (s1, s2, s3, s4, s5, s6, s7, s8, s9, s10)):
             pl.when((i >= lag) & (i < units + lag))(functools.partial(stage, i - lag))
+
+        pl.when(i < units)(lambda: s0_second(i))
 
         @pl.when(i == units // 2)
         def _():
@@ -325,6 +340,32 @@
     for stage, share in ((5, 2), (6, 1), (7, 12), (8, 12), (9, 4)):
         ref = dx.at[:, pl.ds(0, share * width // 32)]
         pltpu.make_async_copy(ref, ref, send.at[stage, 0]).wait()
+
+
+def put_kernel(*refs):
+    count = len(refs) // 2
+    sems = refs[-1]
+    copies = []
+    for i, (src, dst) in enumerate(zip(refs[:count], refs[count:2 * count])):
+        rows = src.shape[0] // PUT
+        for j in range(PUT):
+            at = pl.ds(j * rows, rows)
+            copies.append(pltpu.make_async_copy(src.at[at], dst.at[at], sems.at[i, j]))
+    for c in copies:
+        c.start()
+    for c in copies:
+        c.wait()
+
+
+def put(found):
+    return pl.pallas_call(
+        put_kernel,
+        out_shape=[pltpu.HBM(a.shape, a.dtype) for a in found],
+        in_specs=[pl.BlockSpec(memory_space=pltpu.VMEM)] * len(found),
+        out_specs=[pl.BlockSpec(memory_space=pltpu.HBM)] * len(found),
+        scratch_shapes=[pltpu.SemaphoreType.DMA((len(found), PUT))],
+        compiler_params=pltpu.CompilerParams(vmem_limit_bytes=2**20),
+    )(*found)
 
 
 def solution(mesh):
@@ -339,7 +380,7 @@
         sub = ROWS // side
         out = [pltpu.VMEM(a.shape, a.dtype) for a in (x, w_gate, w_up, w_down)]
         dma = pltpu.SemaphoreType.DMA
-        return tuple(pl.pallas_call(
+        found = pl.pallas_call(
             functools.partial(kernel, side),
             out_shape=out,
             in_specs=[pl.BlockSpec(memory_space=pl.ANY)] * 7,
@@ -353,22 +394,23 @@
                 pltpu.VMEM((2, tokens, TILE), BF16),
                 pltpu.VMEM((2, tokens, TILE), BF16),
                 pltpu.VMEM((SLOTS, ROWS, cu), F32),
-                pltpu.VMEM((SLOTS, ROWS, cw), F32),
+                pltpu.VMEM((SLOTS2, ROWS, cw), F32),
                 pltpu.VMEM((units, 2, ROWS // 2, cw), BF16),
                 pltpu.VMEM((units, 4, ROWS // 2, cw), BF16),
                 pltpu.VMEM((units, 2, sub // 2, cw), BF16),
                 pltpu.VMEM((units, 4, sub // 2, cw), BF16),
                 pltpu.VMEM((units, 2, sub // 2, cw), BF16),
-                dma((3,)),
+                dma((1 + 4 * SPLIT,)),
                 dma((2, 3)),
                 dma((2, 2)),
-                dma((10, 2)),
+                dma((10, FLIGHT)),
                 dma((10, units)),
             ],
             compiler_params=pltpu.CompilerParams(
                 collective_id=0, has_side_effects=True, vmem_limit_bytes=34 * 2**20,
             ),
-        )(x, dy, gate, up, w_gate, w_up, w_down))
+        )(x, dy, gate, up, w_gate, w_up, w_down)
+        return tuple(put(found))
 
     tokens, columns, rows = P("dp", None), P(None, "tp"), P("tp", None)
     return jax.shard_map(

time: 156 us -> 121 us (0.78)
  Pallas kernels: 143 us -> 120 us
  local copies, waits for them, and re-layouts: 12.2 us -> 0 us
    pallas_call x1, Pallas kernels: 143 us -> 110 us  [step(): pl.pallas_call(functools.partial(kernel, side), out_shape=out, in_specs=[...]
    unnamed x4 -> x0, local copies, waits for them, and re-layouts: 12.2 us -> none
    pallas_call x0 -> x1, Pallas kernels: none -> 9.75 us  [put(): pl.pallas_call(put_kernel, out_shape=[pltpu.HBM(a.shape, a.dtype) for a i...]
where the time goes in v2:
time: 121 us; the launch traced here: 120 us
  Pallas kernels  120 us (99%)
    pallas_call x1, Pallas kernels, step(): pl.pallas_call(functools.partial(kernel, side), out_shape=out, in_specs=[...  110 us
    pallas_call x1, Pallas kernels, put(): pl.pallas_call(put_kernel, out_shape=[pltpu.HBM(a.shape, a.dtype) for a i...  9.75 us

profile of v2, /device:TPU:97, one launch (start us, length us, event | category | flops | bytes accessed | tf_op | source)
XLA Modules:
  0.0 120.5 jit_solution(4609980097171872564)
XLA Ops:
  0.6 110.1 %shard_map.102 = (bf16[2048,4096]{1,0:T(8,128)(2,1)S(1)}, bf16[4096,512]{1,0:T(8,128)(2,1)S(1)}, bf16[4096,512]{1,0:T(8,128)(2,1)S(1)}, bf16[512,4096]{1,0:T(8,128)(2,1)S(1)}) custom-call(bf16[2048,4096]{1,0:T(8,128)(2,1)} %x.1, bf16[2048,4096]{1,0:T(8,128)(2,1)} %dy.1, bf16[2048,512]{1,0:T(8,128)(2,1)} %gate.1, bf16[2048,512]{1,0:T(8,128)(2,1)} %up.1, ...), custom_call_target="tpu_custom_call" | custom-call | tf_op jit(solution)/shard_map/pallas_call | solution.py:383
  110.7 9.7 %shard_map.103 = (bf16[2048,4096]{1,0:T(8,128)(2,1)}, bf16[4096,512]{1,0:T(8,128)(2,1)}, bf16[4096,512]{1,0:T(8,128)(2,1)}, bf16[512,4096]{1,0:T(8,128)(2,1)}) custom-call(bf16[2048,4096]{1,0:T(8,128)(2,1)S(1)} %get-tuple-element.8.refs_0_, bf16[4096,512]{1,0:T(8,128)(2,1)S(1)} %get-tuple-element.9.refs_1_, bf16[4096,512]{1,0:T(8,128)(2,1)S(1)} %get-tuple-element.10.refs_2_, ...), custom_call_target="tpu_custom_call" | custom-call | tf_op jit(solution)/shard_map/pallas_call | solution.py:361

commit v3 on v2

--- a/solution.py
+++ b/solution.py
@@ -15,11 +15,12 @@
 ROWS = 256
 SPLIT = 2
 TILE = 256
-LAG = (1, 3, 5, 7, 9, 11, 14, 19, 23, 24)
-SLOTS = 5
+LAG = (1, 3, 6, 8, 10, 12, 14, 18, 23, 24)
+SLOTS = 6
 SLOTS2 = 5
 PUT = 4
 FLIGHT = 4
+VMEM = 35
 
 
 def nt(a, b):
@@ -96,7 +97,7 @@
     load_down.start()
     for c in load_chunk(0):
         c.start()
-    for k in range(SPLIT):
+    def start_blocks(k):
         for h in (1, 0):
             for c in load_block(k, h):
                 c.start()
@@ -133,7 +134,10 @@
 
         @pl.when(r == 0)
         def _():
+            start_blocks(0)
             load_down.wait()
+            for k in range(1, SPLIT):
+                start_blocks(k)
 
         dh = nt(dyb[s], od[...])
         g = gb[s].astype(F32)
@@ -322,10 +326,14 @@
 
     def iteration(i, carry):
         pl.when(i < units)(lambda: s0_first(i))
-        for lag, stage in zip(LAG, (s1, s2, s3, s4, s5, s6, s7, s8, s9, s10)):
+        def link_step(lag, stage):
             pl.when((i >= lag) & (i < units + lag))(functools.partial(stage, i - lag))
 
+        for lag, stage in zip(LAG[:3], (s1, s2, s3)):
+            link_step(lag, stage)
         pl.when(i < units)(lambda: s0_second(i))
+        for lag, stage in zip(LAG[3:], (s4, s5, s6, s7, s8, s9, s10)):
+            link_step(lag, stage)
 
         @pl.when(i == units // 2)
         def _():
@@ -407,7 +415,7 @@
                 dma((10, units)),
             ],
             compiler_params=pltpu.CompilerParams(
-                collective_id=0, has_side_effects=True, vmem_limit_bytes=34 * 2**20,
+                collective_id=0, has_side_effects=True, vmem_limit_bytes=VMEM * 2**20,
             ),
         )(x, dy, gate, up, w_gate, w_up, w_down)
         return tuple(put(found))

time: 121 us -> 117 us (0.967)
  Pallas kernels: 120 us -> 117 us
    pallas_call x1, Pallas kernels: 110 us -> 107 us  [step(): pl.pallas_call(functools.partial(kernel, side), out_shape=out, in_specs=[...]
where the time goes in v3:
time: 117 us
  Pallas kernels  117 us (100%)
    pallas_call x1, Pallas kernels, step(): pl.pallas_call(functools.partial(kernel, side), out_shape=out, in_specs=[...  107 us
    pallas_call x1, Pallas kernels, put(): pl.pallas_call(put_kernel, out_shape=[pltpu.HBM(a.shape, a.dtype) for a i...  9.75 us

profile of v3, /device:TPU:97, one launch (start us, length us, event | category | flops | bytes accessed | tf_op | source)
XLA Modules:
  0.0 117.4 jit_solution(16361441903482401283)
XLA Ops:
  0.6 107.0 %shard_map.102 = (bf16[2048,4096]{1,0:T(8,128)(2,1)S(1)}, bf16[4096,512]{1,0:T(8,128)(2,1)S(1)}, bf16[4096,512]{1,0:T(8,128)(2,1)S(1)}, bf16[512,4096]{1,0:T(8,128)(2,1)S(1)}) custom-call(bf16[2048,4096]{1,0:T(8,128)(2,1)} %x.1, bf16[2048,4096]{1,0:T(8,128)(2,1)} %dy.1, bf16[2048,512]{1,0:T(8,128)(2,1)} %gate.1, bf16[2048,512]{1,0:T(8,128)(2,1)} %up.1, ...), custom_call_target="tpu_custom_call" | custom-call | tf_op jit(solution)/shard_map/pallas_call | solution.py:391
  107.6 9.7 %shard_map.103 = (bf16[2048,4096]{1,0:T(8,128)(2,1)}, bf16[4096,512]{1,0:T(8,128)(2,1)}, bf16[4096,512]{1,0:T(8,128)(2,1)}, bf16[512,4096]{1,0:T(8,128)(2,1)}) custom-call(bf16[2048,4096]{1,0:T(8,128)(2,1)S(1)} %get-tuple-element.8.refs_0_, bf16[4096,512]{1,0:T(8,128)(2,1)S(1)} %get-tuple-element.9.refs_1_, bf16[4096,512]{1,0:T(8,128)(2,1)S(1)} %get-tuple-element.10.refs_2_, ...), custom_call_target="tpu_custom_call" | custom-call | tf_op jit(solution)/shard_map/pallas_call | solution.py:369

commit v4 on v3

--- a/solution.py
+++ b/solution.py
@@ -94,9 +94,9 @@
             pltpu.make_async_copy(w_up.at[rows], ou.at[rows], w_sem.at[at + 1]),
         )
 
-    load_down.start()
     for c in load_chunk(0):
         c.start()
+    load_down.start()
     def start_blocks(k):
         for h in (1, 0):
             for c in load_block(k, h):

time: 117 us -> 117 us (level)
  no operation moved by 1% of the time
where the time goes in v4:
time: 117 us
  Pallas kernels  117 us (100%)
    pallas_call x1, Pallas kernels, step(): pl.pallas_call(functools.partial(kernel, side), out_shape=out, in_specs=[...  107 us
    pallas_call x1, Pallas kernels, put(): pl.pallas_call(put_kernel, out_shape=[pltpu.HBM(a.shape, a.dtype) for a i...  9.75 us

profile of v4, /device:TPU:97, one launch (start us, length us, event | category | flops | bytes accessed | tf_op | source)
XLA Modules:
  0.0 117.3 jit_solution(6782457882813509637)
XLA Ops:
  0.6 106.9 %shard_map.102 = (bf16[2048,4096]{1,0:T(8,128)(2,1)S(1)}, bf16[4096,512]{1,0:T(8,128)(2,1)S(1)}, bf16[4096,512]{1,0:T(8,128)(2,1)S(1)}, bf16[512,4096]{1,0:T(8,128)(2,1)S(1)}) custom-call(bf16[2048,4096]{1,0:T(8,128)(2,1)} %x.1, bf16[2048,4096]{1,0:T(8,128)(2,1)} %dy.1, bf16[2048,512]{1,0:T(8,128)(2,1)} %gate.1, bf16[2048,512]{1,0:T(8,128)(2,1)} %up.1, ...), custom_call_target="tpu_custom_call" | custom-call | tf_op jit(solution)/shard_map/pallas_call | solution.py:391
  107.6 9.7 %shard_map.103 = (bf16[2048,4096]{1,0:T(8,128)(2,1)}, bf16[4096,512]{1,0:T(8,128)(2,1)}, bf16[4096,512]{1,0:T(8,128)(2,1)}, bf16[512,4096]{1,0:T(8,128)(2,1)}) custom-call(bf16[2048,4096]{1,0:T(8,128)(2,1)S(1)} %get-tuple-element.8.refs_0_, bf16[4096,512]{1,0:T(8,128)(2,1)S(1)} %get-tuple-element.9.refs_1_, bf16[4096,512]{1,0:T(8,128)(2,1)S(1)} %get-tuple-element.10.refs_2_, ...), custom_call_target="tpu_custom_call" | custom-call | tf_op jit(solution)/shard_map/pallas_call | solution.py:369
